TPU v7x, 128 devices: a whole 4x4x4 slice. The times are simulated.
128 devices in a mesh: team: 8 (over x, core), inner: 16 (over z, y).
Axes of the slice: x: 4, y: 4, z: 4, core: 2. Of those that a mesh axis runs over, the one named last changes fastest.
Arguments:
- queries: float32 [16384, 1024], P(('team', 'inner')), may hold values from -8 to 8
- passages: float32 [16384, 1024], P(('team', 'inner')), may hold values from -8 to 8
- positive: int32 [16384], P(('team', 'inner')), may hold values from 0 to 16383, as said below
Outputs:
- grad_queries: float32 [16384, 1024], P(('team', 'inner'))
- grad_passages: float32 [16384, 1024], P(('team', 'inner'))
Inputs may be any that keep to these rules, and one draw needn't show every extreme that they name: `positive`: a permutation of the passage indices 0 to 16383.
All inputs are finite; a program needn't handle non-finite values.
Results may differ from a plain program's by a relative error of at most 0.014.
Values may be sent and summed in bfloat16 or wider, within the bound.
A program may use at most 64 MiB of HBM per device.

v0:
```python
import jax
import jax.numpy as jnp
from jax import lax
from jax.sharding import Mesh
from jax.sharding import PartitionSpec as P

INNER = ("inner_0", "inner_1")
TEAM_INNER = ("team", "inner_0", "inner_1")
logit_scale_factor = 20.0
epsilon = 1e-06


def in_order(blocks, dim):
    dims = list(blocks.shape[1:])
    dims[dim] *= blocks.shape[0]
    return jnp.moveaxis(blocks, 0, dim).reshape(dims)


def sent_to_all(x, axis):
    copies = jnp.broadcast_to(x, (lax.axis_size(axis), *x.shape))
    return lax.all_to_all(copies, axis, split_axis=0, concat_axis=0, tiled=True)


def gathered_copies(x, axis, dim):
    return in_order(sent_to_all(x, axis), dim)


def taken_together(x, axis):
    everything = sent_to_all(x, axis)
    return jnp.sum(everything, axis=0)


def summed_rows(terms, axes):
    so_far = terms.astype(jnp.bfloat16)
    for axis in axes:
        so_far = lax.psum_scatter(so_far, axis, scatter_dimension=0, tiled=True)
    return so_far.astype(jnp.float32)


def split_up(x, dim, size):
    dims = x.shape
    blocks = x.reshape(*dims[:dim], size, dims[dim] // size, *dims[dim + 1 :])
    return jnp.moveaxis(blocks, dim, 0)


def summed_on_arrival(x, axis, dim):
    size = lax.axis_size(axis)
    blocks = lax.all_to_all(split_up(x, dim, size), axis, 0, 0, tiled=True)
    return jnp.sum(blocks.astype(jnp.float32), axis=0)


def unit_rows(vectors):
    length = jnp.sqrt(jnp.sum(vectors * vectors, axis=1, keepdims=True) + epsilon)
    return (vectors / length, length)


def finish(unit_vectors, length, grad_raw):
    projection = jnp.sum(unit_vectors * grad_raw, axis=1, keepdims=True)
    return (grad_raw - unit_vectors * projection) / length


def exponent(query_tile_rows, column_block):
    similarity_scores = lax.dot_general(
        query_tile_rows, column_block, (((1,), (1,)), ((), ())), preferred_element_type=jnp.float32
    )
    return jnp.exp(logit_scale_factor * similarity_scores)


def weights(query_tile_rows, column_block, target_block, row_block, column_block_total):
    exponentials = exponent(query_tile_rows, column_block)
    column_ids = lax.iota(jnp.int32, column_block.shape[0])
    is_target = (target_block[:, None] == column_ids[None, :]).astype(jnp.float32)
    combined = (
        exponentials / row_block[:, None]
        + exponentials / column_block_total[None, :]
        - 2.0 * is_target
    )
    return combined.astype(jnp.bfloat16)


def per_device(queries, passages, positive):
    shard_rows = queries.shape[0]
    feature_count = queries.shape[1]
    inner_count = lax.axis_size(INNER)
    team_count = lax.axis_size("team")
    query_unit, query_length = unit_rows(queries)
    passage_unit, passage_length = unit_rows(passages)
    query_round = query_unit.astype(jnp.bfloat16)
    passage_round = passage_unit.astype(jnp.bfloat16)
    team_queries = lax.all_gather(query_round, INNER, axis=0, tiled=True)
    team_targets = lax.all_gather(positive, INNER, axis=0, tiled=True)
    columns = gathered_copies(passage_round, "team", 0)
    team_rows = shard_rows * inner_count
    column_count = shard_rows * team_count
    owner_inner = team_targets % team_rows // shard_rows
    target_column = team_targets // team_rows * shard_rows + team_targets % shard_rows
    target_column = jnp.where(owner_inner == lax.axis_index(INNER), target_column, -1)
    block_rows = shard_rows * min(inner_count, max(1, 512 // shard_rows))
    block_count = team_rows // block_rows
    query_blocks = team_queries.reshape(block_count, block_rows, feature_count)

    def column_sums(running, query_tile_rows):
        exponentials = exponent(query_tile_rows, columns)
        return (running + jnp.sum(exponentials, axis=0), jnp.sum(exponentials, axis=1))

    column_part, row_parts = lax.scan(
        column_sums, jnp.zeros((column_count,), jnp.float32), query_blocks
    )
    row_total = taken_together(row_parts.reshape(team_rows), INNER)
    column_total = lax.psum(column_part, "team")
    query_tile_rows = team_queries
    loss_weight = weights(query_tile_rows, columns, target_column, row_total, column_total)
    query_grad = summed_rows(
        logit_scale_factor * jnp.dot(loss_weight, columns, preferred_element_type=jnp.float32),
        INNER,
    )
    loss_weight = weights(team_queries, columns, target_column, row_total, column_total)
    passage_grad = summed_on_arrival(
        (
            logit_scale_factor
            * lax.dot_general(
                loss_weight,
                team_queries,
                (((0,), (0,)), ((), ())),
                preferred_element_type=jnp.float32,
            )
        ).astype(jnp.bfloat16),
        "team",
        0,
    )
    grad_queries = finish(query_unit, query_length, query_grad)
    grad_passages = finish(passage_unit, passage_length, passage_grad)
    return (grad_queries, grad_passages)


def solution(mesh):
    finer = Mesh(mesh.devices.reshape(mesh.shape["team"], 4, 4), ("team", "inner_0", "inner_1"))
    in_specs = (P(TEAM_INNER, None), P(TEAM_INNER, None), P(TEAM_INNER))
    out_specs = (P(TEAM_INNER, None), P(TEAM_INNER, None))
    return jax.shard_map(
        per_device, mesh=finer, in_specs=in_specs, out_specs=out_specs, check_vma=False
    )
```

profile of v0, /device:TPU:0, one launch (start us, length us, event | category | flops | bytes accessed | tf_op | source)
XLA Modules:
  0.0 193.5 jit_solution(252195710733847977)
XLA Ops:
  7.2 1.2 multiply_reduce_fusion.2
  8.4 1.9 fusion.18
  10.3 1.2 multiply_reduce_fusion.1
  11.4 1.1 fusion.17
  12.6 1.6 broadcast_in_dim.16
  14.2 4.4 %all-to-all-start = ((bf16[8,128,1024]{2,1,0:T(8,128)(2,1)}), bf16[8,128,1024]{2,1,0:T(8,128)(2,1)S(1)}, u32[]{:S(2)}, u32[]{:S(2)}) async-start(bf16[8,128,1024]{2,1,0:T(8,128)(2,1)} %broadcast_in_dim.16), calls=%async_computation | async-start | bytes 4194304 | tf_op jit(solution)/shard_map/all_to_all | solution.py:21
  18.6 22.2 %all-gather = s32[16,1,128]{2,1,0:T(1,128)S(1)} all-gather(s32[1,1,128]{2,1,0:T(1,128)S(1)} %bitcast.32), channel_id=1, replica_groups=mesh['team'=8,'inner_0'=4,'inner_1'=4] {'inner_0','inner_1'}, dimensions={0}, use_global_device_ids=true | all-gather | bytes 8704 | tf_op jit(solution)/shard_map/all_gather | solution.py:91
  40.8 5.0 %all-to-all-done = bf16[8,128,1024]{2,1,0:T(8,128)(2,1)S(1)} async-done(((bf16[8,128,1024]{2,1,0:T(8,128)(2,1)}), bf16[8,128,1024]{2,1,0:T(8,128)(2,1)S(1)}, u32[]{:S(2)}, u32[]{:S(2)}) %all-to-all-start) | async-done | bytes 2097184 | tf_op jit(solution)/shard_map/all_to_all | solution.py:21
  45.8 19.0 %all-gather.3.cloned.1.call-done = bf16[2048,1024]{1,0:T(8,128)(2,1)} async-done(((bf16[128,1024]{1,0:T(8,128)(2,1)}), bf16[2048,1024]{1,0:T(8,128)(2,1)}) %all-gather.3.cloned.1.call-update) | async-done | bytes 4194320 | tf_op jit(solution)/shard_map/all_gather | solution.py:90
  64.7 11.1 %while.13 = (s32[]{:T(128)}, f32[1024]{0:T(1024)S(1)}, f32[4,512]{1,0:T(4,128)S(1)}, bf16[4,512,1024]{2,1,0:T(8,128)(2,1)}, bf16[1024,1024]{1,0:T(8,128)(2,1)S(1)}, /*index=5*/s32[]{:T(128)}, s32[]{:T(128)}) while((s32[]{:T(128)}, f32[1024]{0:T(1024)S(1)}, f32[4,512]{1,0:T(4,128)S(1)}, bf16[4,512,1024]{2,1,0:T(8,128)(2,1)}, ...), condition=%wide.region_5.6_spmd.clone, body=%wide.region_2.5_spmd.clone.sunk | while | flops 1075315200 | bytes 3168359 | solution.py:106
  64.7 2.7 %fusion.29 = (f32[512]{0:T(512)S(1)}, f32[1024]{0:T(1024)S(1)}) fusion(bf16[1024,1024]{1,0:T(8,128)(2,1)S(1)} %get-tuple-element.115, bf16[4,512,1024]{2,1,0:T(8,128)(2,1)} %get-tuple-element.114, s32[]{:T(128)S(6)} %copy.12), kind=kOutput, calls=%fused_computation.1.clone.1 | convolution fusion | flops 1075313152 | bytes 3151876 | tf_op jit(solution)/shard_map/while/body/eval_jaxpr/dot_general | solution.py:63
  67.5 2.7 %fusion.29 = (f32[512]{0:T(512)S(1)}, f32[1024]{0:T(1024)S(1)}) fusion(bf16[1024,1024]{1,0:T(8,128)(2,1)S(1)} %get-tuple-element.115, bf16[4,512,1024]{2,1,0:T(8,128)(2,1)} %get-tuple-element.114, s32[]{:T(128)S(6)} %copy.12), kind=kOutput, calls=%fused_computation.1.clone.1 | convolution fusion | flops 1075313152 | bytes 3151876 | tf_op jit(solution)/shard_map/while/body/eval_jaxpr/dot_general | solution.py:63
  70.2 0.1 dynamic_update_slice.6
  70.3 2.7 %fusion.29 = (f32[512]{0:T(512)S(1)}, f32[1024]{0:T(1024)S(1)}) fusion(bf16[1024,1024]{1,0:T(8,128)(2,1)S(1)} %get-tuple-element.115, bf16[4,512,1024]{2,1,0:T(8,128)(2,1)} %get-tuple-element.114, s32[]{:T(128)S(6)} %copy.12), kind=kOutput, calls=%fused_computation.1.clone.1 | convolution fusion | flops 1075313152 | bytes 3151876 | tf_op jit(solution)/shard_map/while/body/eval_jaxpr/dot_general | solution.py:63
  73.1 2.7 %fusion.29 = (f32[512]{0:T(512)S(1)}, f32[1024]{0:T(1024)S(1)}) fusion(bf16[1024,1024]{1,0:T(8,128)(2,1)S(1)} %get-tuple-element.115, bf16[4,512,1024]{2,1,0:T(8,128)(2,1)} %get-tuple-element.114, s32[]{:T(128)S(6)} %copy.12), kind=kOutput, calls=%fused_computation.1.clone.1 | convolution fusion | flops 1075313152 | bytes 3151876 | tf_op jit(solution)/shard_map/while/body/eval_jaxpr/dot_general | solution.py:63
  75.8 0.1 dynamic_update_slice.6
  75.9 0.7 broadcast_in_dim.36
  76.6 5.3 %all-to-all-start.1 = ((f32[16,1,2048]{2,1,0:T(1,128)}), f32[16,1,2048]{2,1,0:T(1,128)S(1)}, u32[]{:S(2)}, u32[]{:S(2)}) async-start(f32[16,1,2048]{2,1,0:T(1,128)} %broadcast_in_dim.36), calls=%async_computation.1 | async-start | bytes 262144 | tf_op jit(solution)/shard_map/all_to_all | solution.py:21
  82.0 14.4 %psum.7 = f32[1024]{0:T(1024)S(1)} all-reduce(f32[1024]{0:T(1024)S(1)} %get-tuple-element.31), channel_id=1, replica_groups=mesh['team'=8,'inner_0'=4,'inner_1'=4] {'team'}, use_global_device_ids=true, to_apply=%region_7.8 | all-reduce | flops 1024 | bytes 8192 | tf_op jit(solution)/shard_map/psum | solution.py:110
  96.4 0.1 reduce_sum.74
  96.5 7.9 %subtract_convert_fusion = bf16[2048,1024]{1,0:T(8,128)(2,1)S(1)} fusion(bf16[2048,1024]{1,0:T(8,128)(2,1)} %bitcast.34, bf16[1024,1024]{1,0:T(8,128)(2,1)S(1)} %get-tuple-element.125, s32[2048]{0:T(1024)S(1)} %fusion.12, f32[1024]{0:T(1024)S(1)} %psum.7, f32[2048]{0:T(1024)S(1)} %reduce_sum.74), kind=kOutput, calls=%fused_computation.9 | convolution fusion | flops 4311744512 | bytes 10506240 | tf_op jit(solution)/shard_map/dot_general | solution.py:63
  104.4 2.0 %copy-done.3 = bf16[2048,1024]{1,0:T(8,128)(2,1)} copy-done((bf16[2048,1024]{1,0:T(8,128)(2,1)}, bf16[2048,1024]{1,0:T(8,128)(2,1)S(1)}, u32[]{:S(2)}) %copy-start.3) | copy-done | bytes 4194328
  106.4 6.1 %multiply_convert_fusion = bf16[2048,1024]{1,0:T(8,128)(2,1)} fusion(bf16[2048,1024]{1,0:T(8,128)(2,1)S(1)} %subtract_convert_fusion, bf16[1024,1024]{1,0:T(8,128)(2,1)S(1)} %get-tuple-element.125), kind=kOutput, calls=%fused_computation.8 | convolution fusion | flops 4299161600 | bytes 10485760 | tf_op jit(solution)/shard_map/dot_general | solution.py:114
  112.5 9.4 %multiply_convert_fusion.1 = bf16[1024,1024]{1,0:T(8,128)(2,1)} fusion(bf16[2048,1024]{1,0:T(8,128)(2,1)} %copy-done.3, bf16[2048,1024]{1,0:T(8,128)(2,1)} %bitcast.35), kind=kOutput, calls=%fused_computation.12 | convolution fusion | flops 4297064448 | bytes 10485760 | tf_op jit(solution)/shard_map/dot_general | solution.py:121
  121.9 3.7 %all-to-all-start.2 = ((bf16[8,128,1024]{2,1,0:T(8,128)(2,1)}), bf16[8,128,1024]{2,1,0:T(8,128)(2,1)S(1)}, u32[]{:S(2)}, u32[]{:S(2)}) async-start(bf16[8,128,1024]{2,1,0:T(8,128)(2,1)} %bitcast.27), calls=%async_computation.4 | async-start | bytes 4194304 | tf_op jit(solution)/shard_map/all_to_all | solution.py:48
  125.7 32.5 %reduce-scatter.3.cloned.1.call-done = bf16[512,1024]{1,0:T(8,128)(2,1)} async-done(((bf16[2048,1024]{1,0:T(8,128)(2,1)}), bf16[512,1024]{1,0:T(8,128)(2,1)}) %reduce-scatter.3.cloned.1.call-update) | async-done | bytes 1048592 | tf_op jit(solution)/shard_map/reduce_scatter | solution.py:36
  158.2 0.4 convert_reduce_fusion
  158.6 0.2 multiply_reduce_fusion
  158.8 1.0 subtract_divide_fusion
  159.8 24.1 %reduce-scatter.5.cloned.1.call-done = bf16[128,1024]{1,0:T(8,128)(2,1)} async-done(((bf16[512,1024]{1,0:T(8,128)(2,1)}), bf16[128,1024]{1,0:T(8,128)(2,1)}) %reduce-scatter.5.cloned.1.call-update) | async-done | bytes 262160 | tf_op jit(solution)/shard_map/reduce_scatter | solution.py:36
  183.9 1.2 fusion.6
  185.1 1.9 fusion.7
  (27 shorter events, 0.4 us)
Async XLA Ops:
  7.2 57.6 %all-gather.3.cloned.1.call-start = ((), (), s32[]{:S(2)}) async-start(), calls=%async_computation.5 | async-start | bytes 4456448 | tf_op jit(solution)/shard_map/all_gather | solution.py:90
  10.2 8.4 %copy-start.2 = (s32[128]{0:T(128)S(1)}, s32[128]{0:T(128)}, u32[]{:S(2)}) copy-start(s32[128]{0:T(128)} %param.7) | copy-start | bytes 1540
  14.2 31.6 %all-to-all-start = ((bf16[8,128,1024]{2,1,0:T(8,128)(2,1)}), bf16[8,128,1024]{2,1,0:T(8,128)(2,1)S(1)}, u32[]{:S(2)}, u32[]{:S(2)}) async-start(bf16[8,128,1024]{2,1,0:T(8,128)(2,1)} %broadcast_in_dim.16), calls=%async_computation | async-start | bytes 4194304 | tf_op jit(solution)/shard_map/all_to_all | solution.py:21
  76.6 19.8 %all-to-all-start.1 = ((f32[16,1,2048]{2,1,0:T(1,128)}), f32[16,1,2048]{2,1,0:T(1,128)S(1)}, u32[]{:S(2)}, u32[]{:S(2)}) async-start(f32[16,1,2048]{2,1,0:T(1,128)} %broadcast_in_dim.36), calls=%async_computation.1 | async-start | bytes 262144 | tf_op jit(solution)/shard_map/all_to_all | solution.py:21
  81.9 76.3 %reduce-scatter.3.cloned.1.call-start = ((), (), s32[]{:S(2)}) async-start(), calls=%async_computation.6 | async-start | bytes 5242880 | tf_op jit(solution)/shard_map/reduce_scatter | solution.py:36
  104.4 2.0 %copy-start.3 = (bf16[2048,1024]{1,0:T(8,128)(2,1)}, bf16[2048,1024]{1,0:T(8,128)(2,1)S(1)}, u32[]{:S(2)}) copy-start(bf16[2048,1024]{1,0:T(8,128)(2,1)S(1)} %subtract_convert_fusion) | copy-start | bytes 12582916
  121.9 36.7 %copy-start = (f32[128,1024]{1,0:T(8,128)S(1)}, f32[128,1024]{1,0:T(8,128)}, u32[]{:S(2)}) copy-start(f32[128,1024]{1,0:T(8,128)} %param.6) | copy-start | bytes 1572868
  121.9 36.3 %all-to-all-start.2 = ((bf16[8,128,1024]{2,1,0:T(8,128)(2,1)}), bf16[8,128,1024]{2,1,0:T(8,128)(2,1)S(1)}, u32[]{:S(2)}, u32[]{:S(2)}) async-start(bf16[8,128,1024]{2,1,0:T(8,128)(2,1)} %bitcast.27), calls=%async_computation.4 | async-start | bytes 4194304 | tf_op jit(solution)/shard_map/all_to_all | solution.py:48
  125.6 58.3 %copy-start.1 = (f32[128,1024]{1,0:T(8,128)S(1)}, f32[128,1024]{1,0:T(8,128)}, u32[]{:S(2)}) copy-start(f32[128,1024]{1,0:T(8,128)} %param.5) | copy-start | bytes 1572868
  125.6 58.3 %reduce-scatter.5.cloned.1.call-start = ((), (), s32[]{:S(2)}) async-start(), calls=%async_computation.7 | async-start | bytes 1310720 | tf_op jit(solution)/shard_map/reduce_scatter | solution.py:36
Sparse Core Ops, SparseCore 0:
  10.7 54.0 all-gather.2
  112.6 45.5 reduce-scatter.2
  160.6 23.2 reduce-scatter.4
where the time goes:
time: 194 us
  waiting for transfers between devices  80.6 us (42%)
  blocking collectives  36.5 us (19%)
  matrix products  34.2 us (18%)
  between operations  13.9 us (7%)
  starting transfers between devices  13.6 us (7%)
  other arithmetic  10.1 us (5%)
  local copies, waits for them, and re-layouts  4.51 us (2%)
    reduce_scatter x2, waiting for transfers between devices, summed_rows(): so_far = lax.psum_scatter(so_far, axis, scatter_dimension=0, tiled=True)  56.6 us
    all_gather x1, blocking collectives, per_device(): team_targets = lax.all_gather(positive, INNER, axis=0, tiled=True)  22.2 us
    all_gather x1, waiting for transfers between devices, per_device(): team_queries = lax.all_gather(query_round, INNER, axis=0, tiled=True)  19 us
    dot_general x5, matrix products, exponent(): lax.dot_general(query_tile_rows, column_block, (((1,), (1,)), ((), ())),...  18.8 us
    psum x1, blocking collectives, per_device(): column_total = lax.psum(column_part, 'team')  14.4 us
    all_to_all x2, starting transfers between devices, sent_to_all(): return lax.all_to_all(copies, axis, split_axis=0, concat_axis=0, tiled=True)  9.7 us
    dot_general x1, matrix products, per_device(): lax.dot_general(loss_weight, team_queries, (((0,), (0,)), ((), ())), pref...  9.41 us
    dot_general x1, matrix products, per_device(): jnp.dot(loss_weight, columns, preferred_element_type=jnp.float32)  6.06 us
  transfers between devices with their start and end apart: 6, of which 4 were waited for; matrix products, arithmetic and copies ran while one was open for 8% of the time, Pallas kernels for 0%

commit v1 on v0

--- a/solution.py
+++ b/solution.py
@@ -87,7 +87,9 @@
     passage_unit, passage_length = unit_rows(passages)
     query_round = query_unit.astype(jnp.bfloat16)
     passage_round = passage_unit.astype(jnp.bfloat16)
-    team_queries = lax.all_gather(query_round, INNER, axis=0, tiled=True)
+    team_queries = jnp.concatenate(
+        lax.all_to_all(jnp.stack([query_round] * lax.axis_size(INNER)), INNER, 0, 0), axis=0
+    )
     team_targets = lax.all_gather(positive, INNER, axis=0, tiled=True)
     columns = gathered_copies(passage_round, "team", 0)
     team_rows = shard_rows * inner_count

time: 194 us -> 257 us (1.32)
  blocking collectives: 36.5 us -> 86.7 us
  starting transfers between devices: 13.6 us -> 20.9 us
  matrix products: 34.2 us -> 37.6 us
  waiting for transfers between devices: 80.6 us -> 83.9 us
  other arithmetic: 10.1 us -> 7.36 us
    all_gather x1, blocking collectives: 22.2 us -> 73.8 us  [per_device(): team_targets = lax.all_gather(positive, INNER, axis=0, tiled=True)]
    all_to_all x2, waiting for transfers between devices: 5 us -> 26.9 us  [sent_to_all(): return lax.all_to_all(copies, axis, split_axis=0, concat_axis=0, tiled=True)]
    all_gather x1 -> x0, waiting for transfers between devices: 19 us -> none  [per_device(): team_queries = lax.all_gather(query_round, INNER, axis=0, tiled=True)]
    all_to_all x0 -> x1, starting transfers between devices: none -> 8.23 us  [per_device(): lax.all_to_all(jnp.stack([query_round] * lax.axis_size(INNER)), INNER, 0, 0)]
  transfers between devices with their start and end apart: 6 -> 6, of which waited for: 4 -> 3; matrix products, arithmetic and copies ran while one was open for 8% -> 4% of each run, Pallas kernels for 0% -> 0%
where the time goes in v1:
time: 257 us; the launch traced here: 256 us
  blocking collectives  86.7 us (34%)
  waiting for transfers between devices  83.9 us (33%)
  matrix products  37.6 us (15%)
  starting transfers between devices  20.9 us (8%)
  between operations  14.2 us (6%)
  other arithmetic  7.36 us (3%)
  local copies, waits for them, and re-layouts  5.06 us (2%)
    all_gather x1, blocking collectives, per_device(): team_targets = lax.all_gather(positive, INNER, axis=0, tiled=True)  73.8 us
    reduce_scatter x2, waiting for transfers between devices, summed_rows(): so_far = lax.psum_scatter(so_far, axis, scatter_dimension=0, tiled=True)  56.9 us
    all_to_all x2, waiting for transfers between devices, sent_to_all(): return lax.all_to_all(copies, axis, split_axis=0, concat_axis=0, tiled=True)  26.9 us
    dot_general x5, matrix products, exponent(): lax.dot_general(query_tile_rows, column_block, (((1,), (1,)), ((), ())),...  19.9 us
    psum x1, blocking collectives, per_device(): column_total = lax.psum(column_part, 'team')  12.9 us
    dot_general x1, matrix products, per_device(): lax.dot_general(loss_weight, team_queries, (((0,), (0,)), ((), ())), pref...  9.41 us
    all_to_all x2, starting transfers between devices, sent_to_all(): return lax.all_to_all(copies, axis, split_axis=0, concat_axis=0, tiled=True)  8.89 us
    dot_general x1, matrix products, per_device(): jnp.dot(loss_weight, columns, preferred_element_type=jnp.float32)  8.29 us
  transfers between devices with their start and end apart: 6, of which 3 were waited for; matrix products, arithmetic and copies ran while one was open for 4% of the time, Pallas kernels for 0%

profile of v1, /device:TPU:0, one launch (start us, length us, event | category | flops | bytes accessed | tf_op | source)
XLA Modules:
  0.0 255.8 jit_solution(5467014862202731772)
XLA Ops:
  7.2 1.2 multiply_reduce_fusion.1
  8.4 1.1 fusion.17
  9.6 1.6 broadcast_in_dim.16
  11.2 4.4 %all-to-all-start.1 = ((bf16[8,128,1024]{2,1,0:T(8,128)(2,1)}), bf16[8,128,1024]{2,1,0:T(8,128)(2,1)S(1)}, u32[]{:S(2)}, u32[]{:S(2)}) async-start(bf16[8,128,1024]{2,1,0:T(8,128)(2,1)} %broadcast_in_dim.16), calls=%async_computation.1 | async-start | bytes 4194304 | tf_op jit(solution)/shard_map/all_to_all | solution.py:21
  15.6 0.1 multiply_reduce_fusion.2
  15.7 0.1 fusion.18
  15.8 26.9 %all-to-all-done.1 = bf16[8,128,1024]{2,1,0:T(8,128)(2,1)S(1)} async-done(((bf16[8,128,1024]{2,1,0:T(8,128)(2,1)}), bf16[8,128,1024]{2,1,0:T(8,128)(2,1)S(1)}, u32[]{:S(2)}, u32[]{:S(2)}) %all-to-all-start.1) | async-done | bytes 2097184 | tf_op jit(solution)/shard_map/all_to_all | solution.py:21
  42.8 2.5 stack.2
  45.3 8.2 %all-to-all-start = ((bf16[16,128,1024]{2,1,0:T(8,128)(2,1)}), bf16[16,128,1024]{2,1,0:T(8,128)(2,1)}, u32[]{:S(2)}, u32[]{:S(2)}) async-start(bf16[16,128,1024]{2,1,0:T(8,128)(2,1)} %stack.2), calls=%async_computation | async-start | bytes 8388608 | tf_op jit(solution)/shard_map/all_to_all | solution.py:91
  53.5 73.8 %all-gather = s32[16,1,128]{2,1,0:T(1,128)S(1)} all-gather(s32[1,1,128]{2,1,0:T(1,128)S(1)} %bitcast.33), channel_id=1, replica_groups=mesh['team'=8,'inner_0'=4,'inner_1'=4] {'inner_0','inner_1'}, dimensions={0}, use_global_device_ids=true | all-gather | bytes 8704 | tf_op jit(solution)/shard_map/all_gather | solution.py:93
  127.4 10.9 %while.13 = (s32[]{:T(128)}, f32[1024]{0:T(1024)S(1)}, f32[4,512]{1,0:T(4,128)S(1)}, bf16[4,512,1024]{2,1,0:T(8,128)(2,1)}, bf16[1024,1024]{1,0:T(8,128)(2,1)S(1)}, /*index=5*/s32[]{:T(128)}, s32[]{:T(128)}) while((s32[]{:T(128)}, f32[1024]{0:T(1024)S(1)}, f32[4,512]{1,0:T(4,128)S(1)}, bf16[4,512,1024]{2,1,0:T(8,128)(2,1)}, ...), condition=%wide.region_5.6_spmd.clone, body=%wide.region_2.5_spmd.clone.sunk | while | flops 1075315200 | bytes 3168359 | solution.py:108
  127.4 2.7 %fusion.29 = (f32[512]{0:T(512)S(1)}, f32[1024]{0:T(1024)S(1)}) fusion(bf16[1024,1024]{1,0:T(8,128)(2,1)S(1)} %get-tuple-element.115, bf16[4,512,1024]{2,1,0:T(8,128)(2,1)} %get-tuple-element.114, s32[]{:T(128)S(6)} %copy.12), kind=kOutput, calls=%fused_computation.1.clone.1 | convolution fusion | flops 1075313152 | bytes 3151876 | tf_op jit(solution)/shard_map/while/body/eval_jaxpr/dot_general | solution.py:63
  130.0 0.1 dynamic_update_slice.6
  130.1 2.7 %fusion.29 = (f32[512]{0:T(512)S(1)}, f32[1024]{0:T(1024)S(1)}) fusion(bf16[1024,1024]{1,0:T(8,128)(2,1)S(1)} %get-tuple-element.115, bf16[4,512,1024]{2,1,0:T(8,128)(2,1)} %get-tuple-element.114, s32[]{:T(128)S(6)} %copy.12), kind=kOutput, calls=%fused_computation.1.clone.1 | convolution fusion | flops 1075313152 | bytes 3151876 | tf_op jit(solution)/shard_map/while/body/eval_jaxpr/dot_general | solution.py:63
  132.8 0.1 dynamic_update_slice.6
  132.8 2.7 %fusion.29 = (f32[512]{0:T(512)S(1)}, f32[1024]{0:T(1024)S(1)}) fusion(bf16[1024,1024]{1,0:T(8,128)(2,1)S(1)} %get-tuple-element.115, bf16[4,512,1024]{2,1,0:T(8,128)(2,1)} %get-tuple-element.114, s32[]{:T(128)S(6)} %copy.12), kind=kOutput, calls=%fused_computation.1.clone.1 | convolution fusion | flops 1075313152 | bytes 3151876 | tf_op jit(solution)/shard_map/while/body/eval_jaxpr/dot_general | solution.py:63
  135.6 2.7 %fusion.29 = (f32[512]{0:T(512)S(1)}, f32[1024]{0:T(1024)S(1)}) fusion(bf16[1024,1024]{1,0:T(8,128)(2,1)S(1)} %get-tuple-element.115, bf16[4,512,1024]{2,1,0:T(8,128)(2,1)} %get-tuple-element.114, s32[]{:T(128)S(6)} %copy.12), kind=kOutput, calls=%fused_computation.1.clone.1 | convolution fusion | flops 1075313152 | bytes 3151876 | tf_op jit(solution)/shard_map/while/body/eval_jaxpr/dot_general | solution.py:63
  138.3 0.7 broadcast_in_dim.36
  139.0 4.5 %all-to-all-start.2 = ((f32[16,1,2048]{2,1,0:T(1,128)}), f32[16,1,2048]{2,1,0:T(1,128)S(1)}, u32[]{:S(2)}, u32[]{:S(2)}) async-start(f32[16,1,2048]{2,1,0:T(1,128)} %broadcast_in_dim.36), calls=%async_computation.2 | async-start | bytes 262144 | tf_op jit(solution)/shard_map/all_to_all | solution.py:21
  143.6 12.9 %psum.7 = f32[1024]{0:T(1024)S(1)} all-reduce(f32[1024]{0:T(1024)S(1)} %get-tuple-element.31), channel_id=1, replica_groups=mesh['team'=8,'inner_0'=4,'inner_1'=4] {'team'}, use_global_device_ids=true, to_apply=%region_7.8 | all-reduce | flops 1024 | bytes 8192 | tf_op jit(solution)/shard_map/psum | solution.py:112
  156.5 0.1 reduce_sum.74
  156.6 9.3 %subtract_convert_fusion = bf16[2048,1024]{1,0:T(8,128)(2,1)} fusion(bf16[2048,1024]{1,0:T(8,128)(2,1)} %bitcast, bf16[1024,1024]{1,0:T(8,128)(2,1)S(1)} %get-tuple-element.126, s32[2048]{0:T(1024)S(1)} %fusion.12, f32[1024]{0:T(1024)S(1)} %psum.7, f32[2048]{0:T(1024)S(1)} %reduce_sum.74), kind=kOutput, calls=%fused_computation.9 | convolution fusion | flops 4311744512 | bytes 10506240 | tf_op jit(solution)/shard_map/dot_general | solution.py:63
  165.9 8.3 %multiply_convert_fusion = bf16[2048,1024]{1,0:T(8,128)(2,1)} fusion(bf16[2048,1024]{1,0:T(8,128)(2,1)} %subtract_convert_fusion, bf16[1024,1024]{1,0:T(8,128)(2,1)S(1)} %get-tuple-element.126), kind=kOutput, calls=%fused_computation.8 | convolution fusion | flops 4299161600 | bytes 10485760 | tf_op jit(solution)/shard_map/dot_general | solution.py:116
  174.2 9.4 %multiply_convert_fusion.1 = bf16[1024,1024]{1,0:T(8,128)(2,1)} fusion(bf16[2048,1024]{1,0:T(8,128)(2,1)} %subtract_convert_fusion, bf16[2048,1024]{1,0:T(8,128)(2,1)} %bitcast), kind=kOutput, calls=%fused_computation.12 | convolution fusion | flops 4297064448 | bytes 10485760 | tf_op jit(solution)/shard_map/dot_general | solution.py:123
  183.6 3.7 %all-to-all-start.3 = ((bf16[8,128,1024]{2,1,0:T(8,128)(2,1)}), bf16[8,128,1024]{2,1,0:T(8,128)(2,1)S(1)}, u32[]{:S(2)}, u32[]{:S(2)}) async-start(bf16[8,128,1024]{2,1,0:T(8,128)(2,1)} %bitcast.28), calls=%async_computation.5 | async-start | bytes 4194304 | tf_op jit(solution)/shard_map/all_to_all | solution.py:48
  187.4 32.8 %reduce-scatter.3.cloned.1.call-done = bf16[512,1024]{1,0:T(8,128)(2,1)} async-done(((bf16[2048,1024]{1,0:T(8,128)(2,1)}), bf16[512,1024]{1,0:T(8,128)(2,1)}) %reduce-scatter.3.cloned.1.call-update) | async-done | bytes 1048592 | tf_op jit(solution)/shard_map/reduce_scatter | solution.py:36
  220.2 0.3 convert_reduce_fusion
  220.6 0.2 multiply_reduce_fusion
  220.8 1.0 subtract_divide_fusion
  221.8 24.1 %reduce-scatter.5.cloned.1.call-done = bf16[128,1024]{1,0:T(8,128)(2,1)} async-done(((bf16[512,1024]{1,0:T(8,128)(2,1)}), bf16[128,1024]{1,0:T(8,128)(2,1)}) %reduce-scatter.5.cloned.1.call-update) | async-done | bytes 262160 | tf_op jit(solution)/shard_map/reduce_scatter | solution.py:36
  245.9 1.2 fusion.6
  247.1 1.9 fusion.7
  (25 shorter events, 0.3 us)
Async XLA Ops:
  7.2 8.4 %copy-start.1 = (f32[128,1024]{1,0:T(8,128)S(1)}, f32[128,1024]{1,0:T(8,128)}, u32[]{:S(2)}) copy-start(f32[128,1024]{1,0:T(8,128)} %param.5) | copy-start | bytes 1572868
  11.2 31.6 %all-to-all-start.1 = ((bf16[8,128,1024]{2,1,0:T(8,128)(2,1)}), bf16[8,128,1024]{2,1,0:T(8,128)(2,1)S(1)}, u32[]{:S(2)}, u32[]{:S(2)}) async-start(bf16[8,128,1024]{2,1,0:T(8,128)(2,1)} %broadcast_in_dim.16), calls=%async_computation.1 | async-start | bytes 4194304 | tf_op jit(solution)/shard_map/all_to_all | solution.py:21
  45.3 8.3 %copy-start.2 = (s32[128]{0:T(128)S(1)}, s32[128]{0:T(128)}, u32[]{:S(2)}) copy-start(s32[128]{0:T(128)} %param.7) | copy-start | bytes 1540
  45.3 82.1 %all-to-all-start = ((bf16[16,128,1024]{2,1,0:T(8,128)(2,1)}), bf16[16,128,1024]{2,1,0:T(8,128)(2,1)}, u32[]{:S(2)}, u32[]{:S(2)}) async-start(bf16[16,128,1024]{2,1,0:T(8,128)(2,1)} %stack.2), calls=%async_computation | async-start | bytes 8388608 | tf_op jit(solution)/shard_map/all_to_all | solution.py:91
  139.0 17.5 %all-to-all-start.2 = ((f32[16,1,2048]{2,1,0:T(1,128)}), f32[16,1,2048]{2,1,0:T(1,128)S(1)}, u32[]{:S(2)}, u32[]{:S(2)}) async-start(f32[16,1,2048]{2,1,0:T(1,128)} %broadcast_in_dim.36), calls=%async_computation.2 | async-start | bytes 262144 | tf_op jit(solution)/shard_map/all_to_all | solution.py:21
  143.5 76.7 %reduce-scatter.3.cloned.1.call-start = ((), (), s32[]{:S(2)}) async-start(), calls=%async_computation.6 | async-start | bytes 5242880 | tf_op jit(solution)/shard_map/reduce_scatter | solution.py:36
  183.6 37.0 %copy-start = (f32[128,1024]{1,0:T(8,128)S(1)}, f32[128,1024]{1,0:T(8,128)}, u32[]{:S(2)}) copy-start(f32[128,1024]{1,0:T(8,128)} %param.6) | copy-start | bytes 1572868
  183.6 36.6 %all-to-all-start.3 = ((bf16[8,128,1024]{2,1,0:T(8,128)(2,1)}), bf16[8,128,1024]{2,1,0:T(8,128)(2,1)S(1)}, u32[]{:S(2)}, u32[]{:S(2)}) async-start(bf16[8,128,1024]{2,1,0:T(8,128)(2,1)} %bitcast.28), calls=%async_computation.5 | async-start | bytes 4194304 | tf_op jit(solution)/shard_map/all_to_all | solution.py:48
  187.3 58.6 %reduce-scatter.5.cloned.1.call-start = ((), (), s32[]{:S(2)}) async-start(), calls=%async_computation.7 | async-start | bytes 1310720 | tf_op jit(solution)/shard_map/reduce_scatter | solution.py:36
Sparse Core Ops, SparseCore 0:
  174.3 45.8 reduce-scatter.2
  222.6 23.2 reduce-scatter.4
